TPU v7x, 32 devices: a whole 2x2x4 slice. The times are simulated.
32 devices in a mesh: gx: 2 (over y), gy: 4 (over z), gz: 4 (over x, core).
Axes of the slice: x: 2, y: 2, z: 4, core: 2. Of those that a mesh axis runs over, the one named last changes fastest.
Arguments:
- kappa_sq: float32 [32, 64, 512], P('gx', 'gz', 'gy'), may hold values from 0.004 to 0.4
- probe_bits: int32 [4, 32, 64, 512], P(None, 'gx', 'gz', 'gy'), may hold values from 0 to 1
Outputs:
- solution: float32 [4, 32, 64, 512], P(None, 'gx', 'gz', 'gy')
- relative_residual: float32 [4], replicated
All inputs are finite; a program needn't handle non-finite values.
Results may differ from a plain program's by a relative error of at most 0.0001.
Values sent between devices are 32-bit elements; how exact they have to be, the bound alone decides.
A program may use at most 128 MiB of HBM per device.

v0:
```python
import jax
import jax.numpy as jnp
from jax import lax
from jax.sharding import PartitionSpec as P

LEVELS = 3
COARSE_SWEEPS = 8
ITERS = 2
damping = 0.8


def extended(block, sides, width):
    for axis, dim in sides:
        count = lax.axis_size(axis)
        forward = [(i, i + 1) for i in range(count - 1)]
        backward = [(target, source) for source, target in forward]
        low = lax.ppermute(
            lax.slice_in_dim(block, block.shape[dim] - width, None, axis=dim), axis, forward
        )
        high = lax.ppermute(lax.slice_in_dim(block, 0, width, axis=dim), axis, backward)
        block = jnp.concatenate([low, block, high], axis=dim)
    return block


def neighbours(padded):
    along_first = padded[..., 2:, 1:-1, 1:-1] + padded[..., :-2, 1:-1, 1:-1]
    along_second = padded[..., 1:-1, 2:, 1:-1] + padded[..., 1:-1, :-2, 1:-1]
    along_third = padded[..., 1:-1, 1:-1, 2:] + padded[..., 1:-1, 1:-1, :-2]
    return along_first + along_second + along_third


def coarsen(field):
    leading = field.shape[:-3]
    cells_first, cells_second, cells_third = field.shape[-3:]
    grouped = field.reshape(
        leading + (cells_first // 2, 2, cells_second // 2, 2, cells_third // 2, 2)
    )
    return jnp.mean(grouped, axis=(-5, -3, -1))


def refine(field):
    leading = field.shape[:-3]
    cells_first, cells_second, cells_third = field.shape[-3:]
    spread = field.reshape(leading + (cells_first, 1, cells_second, 1, cells_third, 1))
    spread = jnp.broadcast_to(spread, leading + (cells_first, 2, cells_second, 2, cells_third, 2))
    return spread.reshape(leading + (cells_first * 2, cells_second * 2, cells_third * 2))


def level_faces(field, grid_level):
    if grid_level == 0:
        return extended(field, (("gx", 1), ("gy", 3), ("gz", 2)), 1)
    return extended(field, (("gx", 1), ("gy", 3), ("gz", 2)), 1)


def operate(field, diagonal, coupling, grid_level):
    return diagonal * field - coupling * neighbours(level_faces(field, grid_level))


def jacobi_sweep(field, rhs_field, diagonal, coupling, grid_level):
    return field + damping * (rhs_field - operate(field, diagonal, coupling, grid_level)) / diagonal


def assemble(gathered):
    count_x = lax.axis_size("gx")
    count_y = lax.axis_size("gy")
    count_z = lax.axis_size("gz")
    leading = gathered.shape[1:-3]
    cells_first, cells_second, cells_third = gathered.shape[-3:]
    lead_count = len(leading)
    blocks = gathered.reshape(
        (count_x, count_y, count_z) + leading + (cells_first, cells_second, cells_third)
    )
    permutation = tuple(range(3, 3 + lead_count)) + (
        0,
        3 + lead_count,
        2,
        4 + lead_count,
        1,
        5 + lead_count,
    )
    blocks = jnp.transpose(blocks, permutation)
    return blocks.reshape(
        leading + (count_x * cells_first, count_z * cells_second, count_y * cells_third)
    )


def local_dot(first_field, second_field):
    return jnp.sum(first_field * second_field, axis=(1, 2, 3))


def expand(values):
    return values[:, None, None, None]


def per_device(kappa_sq, probe_bits):
    diagonals = []
    couplings = []
    coef_field = kappa_sq
    for grid_level in range(LEVELS + 1):
        if grid_level > 0:
            coef_field = coarsen(coef_field)
        coupling = 0.25**grid_level
        diagonals.append(coef_field + 6.0 * coupling)
        couplings.append(coupling)
    global_diag = assemble(
        lax.all_gather(diagonals[LEVELS][None], ("gx", "gy", "gz"), axis=0, tiled=True)
    )

    def coarsest(rhs_field):
        diagonal = diagonals[LEVELS]
        coupling = couplings[LEVELS]
        global_rhs = assemble(
            lax.all_gather(rhs_field[None], ("gx", "gy", "gz"), axis=0, tiled=True)
        )
        field = damping * global_rhs / global_diag
        for sweep_index in range(COARSE_SWEEPS - 1):
            padded = jnp.pad(field, ((0, 0), (1, 1), (1, 1), (1, 1)))
            field = (
                field
                + damping
                * (global_rhs - (global_diag * field - coupling * neighbours(padded)))
                / global_diag
            )
        probes, block_x, block_z, block_y = rhs_field.shape
        zero_index = jnp.zeros((), jnp.int32)
        starts = (
            zero_index,
            lax.axis_index("gx") * block_x,
            lax.axis_index("gz") * block_z,
            lax.axis_index("gy") * block_y,
        )
        return lax.dynamic_slice(field, starts, (probes, block_x, block_z, block_y))

    def vcycle(rhs_field, grid_level):
        if grid_level == LEVELS:
            return coarsest(rhs_field)
        diagonal = diagonals[grid_level]
        coupling = couplings[grid_level]
        field = damping * rhs_field / diagonal
        field = jacobi_sweep(field, rhs_field, diagonal, coupling, grid_level)
        remainder = rhs_field - operate(field, diagonal, coupling, grid_level)
        field = field + refine(vcycle(coarsen(remainder), grid_level + 1))
        field = jacobi_sweep(field, rhs_field, diagonal, coupling, grid_level)
        return jacobi_sweep(field, rhs_field, diagonal, coupling, grid_level)

    right_side = 2.0 * probe_bits.astype(jnp.float32) - 1.0
    solution = jnp.zeros_like(right_side)
    residual = right_side
    fine_diag = diagonals[0]

    def precond_sum(first_field, second_field):
        return lax.psum(local_dot(first_field, second_field), ("gx", "gy", "gz"))

    precond = vcycle(residual, 0)
    precond_dot = precond_sum(residual, precond)
    search = precond
    for iteration in range(ITERS):
        operated = operate(search, fine_diag, 1.0, 0)
        step_size = precond_dot / lax.psum(local_dot(search, operated), ("gx", "gy", "gz"))
        solution = solution + expand(step_size) * search
        residual = residual - expand(step_size) * operated
        if iteration + 1 < ITERS:
            precond = vcycle(residual, 0)
            next_dot = precond_sum(residual, precond)
            search = precond + expand(next_dot / precond_dot) * search
            precond_dot = next_dot
    squares = lax.psum(local_dot(residual, residual), ("gx", "gy", "gz"))
    cell_total = (
        probe_bits.shape[1]
        * probe_bits.shape[2]
        * probe_bits.shape[3]
        * lax.axis_size("gx")
        * lax.axis_size("gy")
        * lax.axis_size("gz")
    )
    return (solution, jnp.sqrt(squares / cell_total))


def solution(mesh):
    return jax.shard_map(
        per_device,
        mesh=mesh,
        in_specs=(P("gx", "gz", "gy"), P(None, "gx", "gz", "gy")),
        out_specs=(P(None, "gx", "gz", "gy"), P()),
        check_vma=False,
    )
```

profile of v0, /device:TPU:0, one launch (start us, length us, event | category | flops | bytes accessed | tf_op | source)
XLA Modules:
  0.0 1080.8 jit_solution(16804115378510842129)
XLA Ops:
  2.7 4.9 collective-permute-start.1
  9.2 4.2 collective-permute-done
  16.0 4.5 collective-permute-start.2
  33.6 4.2 collective-permute-done.6
  40.4 4.8 collective-permute-start.8
  45.2 9.7 reshape.124
  69.1 8.8 copy.1882
  77.9 11.7 %reduce_sum.126 = f32[4,8,8,64]{0,3,2,1:T(8,128)S(1)} reduce(f32[4,8,2,8,2,64,2]{0,6,5,4,3,2,1:T(2,128)} %bitcast.21, f32[]{:T(128)} %constant.28.clone.1), dimensions={2,4,6}, to_apply=%region_0.0 | reduce | flops 114688 | bytes 589828 | tf_op jit(solution)/shard_map/reduce_sum | solution.py:38
  99.1 4.6 collective-permute-start.14
  117.1 4.3 collective-permute-done.18
  122.8 4.7 collective-permute-start.20
  147.8 4.4 collective-permute-start.26
  154.1 4.4 collective-permute-done.27
  168.1 47.4 %all-gather.1 = f32[64,2,16]{2,1,0:T(2,128)S(1)} all-gather(f32[2,2,16]{2,1,0:T(2,128)S(1)} %multiply_add_fusion.3), channel_id=3, replica_groups=mesh['gx'=2,'gy'=4,'gz'=4] {'gx','gy','gz'}, dimensions={0}, use_global_device_ids=true | all-gather | bytes 8448 | tf_op jit(solution)/shard_map/all_gather | solution.py:106
  219.1 4.2 collective-permute-done.33
  230.6 40.5 %all-gather = f32[128,2,2,16]{3,2,1,0:T(2,128)S(1)} all-gather(f32[4,2,2,16]{3,2,1,0:T(2,128)S(1)} %copy.1905), channel_id=2, replica_groups=mesh['gx'=2,'gy'=4,'gz'=4] {'gx','gy','gz'}, dimensions={0}, use_global_device_ids=true | all-gather | bytes 33792 | tf_op jit(solution)/shard_map/all_gather | solution.py:113
  283.4 4.3 collective-permute-done.39
  298.5 4.3 collective-permute-done.42
  306.0 4.3 collective-permute-done.45
  328.2 4.6 collective-permute-start.50
  337.1 4.6 collective-permute-start.53
  351.9 4.7 collective-permute-start.56
  361.0 5.0 collective-permute-start.59
  369.5 7.8 broadcast_in_dim.14
  377.3 10.0 copy.1931
  390.9 4.2 collective-permute-done.60
  397.7 4.7 collective-permute-start.62
  405.1 4.3 collective-permute-start.65
  410.8 5.8 collective-permute-done.64
  420.8 4.2 collective-permute-done.66
  427.6 4.8 collective-permute-start.68
  446.8 4.2 collective-permute-done.72
  453.6 4.8 collective-permute-start.74
  469.7 41.7 %all-reduce.14 = (f32[4]{0:T(128)S(1)}, f32[4]{0:T(128)S(1)}) all-reduce(f32[4]{0:T(128)S(1)} %get-tuple-element.13, f32[4]{0:T(128)S(1)} %get-tuple-element.12), channel_id=1, replica_groups=mesh['gx'=2,'gy'=4,'gz'=4] {'gx','gy','gz'}, use_global_device_ids=true, to_apply=%region_7.8 | all-reduce | flops 8 | bytes 64 | tf_op jit(solution)/shard_map/psum | solution.py:152
  517.6 4.2 collective-permute-done.78
  524.4 4.5 collective-permute-start.80
  543.3 4.2 collective-permute-done.84
  550.0 4.8 collective-permute-start.86
  566.8 8.8 copy.1982
  575.7 13.1 %reduce_sum.134 = f32[4,8,8,64]{0,3,2,1:T(8,128)} reduce(f32[4,8,2,8,2,64,2]{0,6,5,4,3,2,1:T(2,128)} %bitcast.23, f32[]{:T(128)} %constant.28.clone.1), dimensions={2,4,6}, to_apply=%region_10.11 | reduce | flops 114688 | bytes 589828 | tf_op jit(solution)/shard_map/reduce_sum | solution.py:38
  594.2 4.2 collective-permute-done.90
  599.8 4.9 collective-permute-start.92
  623.4 4.7 collective-permute-start.98
  652.0 4.4 collective-permute-start.104
  658.3 4.4 collective-permute-done.105
  687.1 4.3 collective-permute-done.111
  701.8 44.2 %all-gather.2 = f32[128,2,2,16]{3,2,1,0:T(2,128)S(1)} all-gather(f32[4,2,2,16]{3,2,1,0:T(2,128)S(1)} %copy.2005), channel_id=4, replica_groups=mesh['gx'=2,'gy'=4,'gz'=4] {'gx','gy','gz'}, dimensions={0}, use_global_device_ids=true | all-gather | bytes 33792 | tf_op jit(solution)/shard_map/all_gather | solution.py:113
  760.9 4.3 collective-permute-done.117
  787.3 4.3 collective-permute-done.123
  815.0 4.6 collective-permute-start.128
  831.2 4.2 collective-permute-done.132
  836.9 5.0 collective-permute-start.134
  853.7 8.9 broadcast_in_dim.17
  862.6 10.0 copy.2029
  876.2 4.2 collective-permute-done.138
  883.0 5.0 collective-permute-start.140
  893.9 5.8 collective-permute-done.142
  904.0 4.2 collective-permute-done.144
  910.7 5.1 collective-permute-start.146
  926.9 41.6 %psum.37 = f32[4]{0:T(128)S(1)} all-reduce(f32[4]{0:T(128)S(1)} %get-tuple-element.18), channel_id=1, replica_groups=mesh['gx'=2,'gy'=4,'gz'=4] {'gx','gy','gz'}, use_global_device_ids=true, to_apply=%region_14.15 | all-reduce | flops 4 | bytes 32 | tf_op jit(solution)/shard_map/psum | solution.py:152
  974.4 4.2 collective-permute-done.150
  981.2 4.5 collective-permute-start.152
  996.1 41.6 %psum.38 = f32[4]{0:T(128)S(1)} all-reduce(f32[4]{0:T(128)S(1)} %get-tuple-element.16), channel_id=1, replica_groups=mesh['gx'=2,'gy'=4,'gz'=4] {'gx','gy','gz'}, use_global_device_ids=true, to_apply=%region_16.17 | all-reduce | flops 4 | bytes 32 | tf_op jit(solution)/shard_map/psum | solution.py:159
  1038.8 41.2 %psum.39 = f32[4]{0:T(128)S(1)} all-reduce(f32[4]{0:T(128)S(1)} %get-tuple-element.199), channel_id=1, replica_groups=mesh['gx'=2,'gy'=4,'gz'=4] {'gx','gy','gz'}, use_global_device_ids=true, to_apply=%region_18.19 | all-reduce | flops 4 | bytes 32 | tf_op jit(solution)/shard_map/psum | solution.py:167
  (655 shorter events, 471.4 us)
Async XLA Ops:
  2.7 6.5 collective-permute-start.1
  14.2 6.3 collective-permute-start.3
  16.0 6.1 collective-permute-start.2
  38.6 20.4 %collective-permute-start.9 = (f32[4,18,16,1]{1,2,3,0:T(8,128)S(1)}, f32[4,18,16,1]{1,2,3,0:T(8,128)S(1)}, u32[]{:S(2)}, u32[]{:S(2)}) collective-permute-start(f32[4,18,16,1]{1,2,3,0:T(8,128)S(1)} %copy.1873), channel_id=1, source_target_pairs={{4,0},{8,4},{12,8},{5,1},{9,5},{13,9},{6,2},{10,6},{14,10},{7,3},{... | collective-permute-start | bytes 13832 | tf_op jit(solution)/shard_map/ppermute | solution.py:20
  40.4 19.1 %collective-permute-start.8 = (f32[4,18,16,1]{1,2,3,0:T(8,128)S(1)}, f32[4,18,16,1]{1,2,3,0:T(8,128)S(1)}, u32[]{:S(2)}, u32[]{:S(2)}) collective-permute-start(f32[4,18,16,1]{1,2,3,0:T(8,128)S(1)} %copy.1872), channel_id=1, source_target_pairs={{0,4},{4,8},{8,12},{1,5},{5,9},{9,13},{2,6},{6,10},{10,14},{3,7},{... | collective-permute-start | bytes 13832 | tf_op jit(solution)/shard_map/ppermute | solution.py:17
  97.8 8.1 collective-permute-start.15
  99.1 8.5 collective-permute-start.14
  121.5 8.8 collective-permute-start.21
  122.8 8.7 collective-permute-start.20
  141.5 6.2 collective-permute-start.24
  147.8 6.3 collective-permute-start.26
  152.2 6.3 collective-permute-start.27
  165.2 50.5 %collective-permute-start.31 = (f32[4,1,4,32]{0,3,2,1:T(8,128)S(1)}, f32[4,1,4,32]{0,3,2,1:T(8,128)S(1)}, u32[]{:S(2)}, u32[]{:S(2)}) collective-permute-start(f32[4,1,4,32]{0,3,2,1:T(8,128)S(1)} %get-tuple-element.127), channel_id=1, source_target_pairs={{0,16},{1,17},{2,18},{3,19},{4,20},{5,21},{6,22},{7,23},{8,24},{9,... | collective-permute-start | bytes 6152 | tf_op jit(solution)/shard_map/ppermute | solution.py:17
  166.8 49.0 %collective-permute-start.30 = (f32[4,1,4,32]{0,3,2,1:T(8,128)S(1)}, f32[4,1,4,32]{0,3,2,1:T(8,128)S(1)}, u32[]{:S(2)}, u32[]{:S(2)}) collective-permute-start(f32[4,1,4,32]{0,3,2,1:T(8,128)S(1)} %get-tuple-element.128), channel_id=1, source_target_pairs={{16,0},{17,1},{18,2},{19,3},{20,4},{21,5},{22,6},{23,7},{24,8},{25... | collective-permute-start | bytes 6152 | tf_op jit(solution)/shard_map/ppermute | solution.py:20
  217.3 6.0 collective-permute-start.33
  273.9 6.2 collective-permute-start.36
  281.7 6.0 collective-permute-start.39
  296.0 6.7 collective-permute-start.42
  304.2 6.0 collective-permute-start.45
  326.9 7.2 collective-permute-start.51
  328.2 7.4 collective-permute-start.50
  350.6 7.4 collective-permute-start.57
  351.9 7.5 collective-permute-start.56
  359.7 6.3 collective-permute-start.58
  395.9 6.5 collective-permute-start.63
  397.7 6.3 collective-permute-start.62
  409.4 7.2 collective-permute-start.64
  425.8 6.6 collective-permute-start.69
  427.6 6.4 collective-permute-start.68
  451.8 6.6 collective-permute-start.75
  453.6 6.4 collective-permute-start.74
  522.6 6.3 collective-permute-start.81
  524.4 6.1 collective-permute-start.80
  548.2 6.6 collective-permute-start.87
  550.0 6.4 collective-permute-start.86
  598.5 8.4 collective-permute-start.93
  599.8 8.8 collective-permute-start.92
  622.1 8.8 collective-permute-start.99
  623.4 8.7 collective-permute-start.98
  645.0 6.2 collective-permute-start.102
  652.0 6.3 collective-permute-start.104
  656.4 6.3 collective-permute-start.105
  663.8 6.9 collective-permute-start.106
  665.1 6.2 collective-permute-start.107
  674.4 6.2 collective-permute-start.108
  685.3 6.0 collective-permute-start.111
  692.4 6.2 collective-permute-start.112
  750.9 6.2 collective-permute-start.114
  766.3 7.0 collective-permute-start.118
  767.6 6.4 collective-permute-start.119
  777.0 6.2 collective-permute-start.120
  792.7 6.9 collective-permute-start.124
  794.0 6.2 collective-permute-start.125
  813.7 7.2 collective-permute-start.129
  815.0 7.4 collective-permute-start.128
  835.6 9.1 collective-permute-start.135
  836.9 8.9 collective-permute-start.134
  881.2 6.8 collective-permute-start.141
  883.0 6.6 collective-permute-start.140
  892.5 7.2 collective-permute-start.142
  908.9 6.8 collective-permute-start.147
  910.7 6.4 collective-permute-start.146
  979.4 6.3 collective-permute-start.153
  981.2 6.1 collective-permute-start.152
  (112 other events, 723.4 us)
where the time goes:
time: 1090 us; the launch traced here: 1080 us
  starting transfers between devices  340 us (31%)
  blocking collectives  298 us (27%)
  waiting for transfers between devices  234 us (21%)
  local copies, waits for them, and re-layouts  131 us (12%)
  other arithmetic  74.1 us (7%)
    ppermute x78, starting transfers between devices, extended(): lax.ppermute(lax.slice_in_dim(block, block.shape[dim] - width, None, axis...  238 us
    ppermute x78, waiting for transfers between devices, extended(): lax.ppermute(lax.slice_in_dim(block, 0, width, axis=dim), axis, backward)  195 us
    ppermute x78, starting transfers between devices, extended(): lax.ppermute(lax.slice_in_dim(block, 0, width, axis=dim), axis, backward)  101 us
    all_gather x2, blocking collectives, coarsest(): lax.all_gather(rhs_field[None], ('gx', 'gy', 'gz'), axis=0, tiled=True)  84.7 us
    psum x2, blocking collectives, precond_sum(): return lax.psum(local_dot(first_field, second_field), ('gx', 'gy', 'gz'))  83.3 us
    all_gather x1, blocking collectives, per_device(): lax.all_gather(diagonals[LEVELS][None], ('gx', 'gy', 'gz'), axis=0, tiled...  47.4 us
    psum x1, blocking collectives, per_device(): lax.psum(local_dot(search, operated), ('gx', 'gy', 'gz'))  41.6 us
    psum x1, blocking collectives, per_device(): squares = lax.psum(local_dot(residual, residual), ('gx', 'gy', 'gz'))  41.2 us
  transfers between devices with their start and end apart: 156, of which 111 were waited for; matrix products, arithmetic and copies ran while one was open for 3% of the time, Pallas kernels for 0%

commit v1 on v0

--- a/solution.py
+++ b/solution.py
@@ -149,7 +149,9 @@
     fine_diag = diagonals[0]
 
     def precond_sum(first_field, second_field):
-        return lax.psum(local_dot(first_field, second_field), ("gx", "gy", "gz"))
+        return jnp.sum(
+            lax.all_gather(local_dot(first_field, second_field), ("gx", "gy", "gz")), axis=0
+        )
 
     precond = vcycle(residual, 0)
     precond_dot = precond_sum(residual, precond)

time: 1090 us -> 1090 us (level)
  waiting for transfers between devices: 234 us -> 198 us
  starting transfers between devices: 340 us -> 369 us
    unnamed x0 -> x2, blocking collectives: none -> 91.2 us
    psum x2 -> x0, blocking collectives: 83.3 us -> none  [precond_sum(): return lax.psum(local_dot(first_field, second_field), ('gx', 'gy', 'gz'))]
    ppermute x78, waiting for transfers between devices: 195 us -> 135 us  [extended(): lax.ppermute(lax.slice_in_dim(block, 0, width, axis=dim), axis, backward)]
    ppermute x78, starting transfers between devices: 238 us -> 268 us  [extended(): lax.ppermute(lax.slice_in_dim(block, block.shape[dim] - width, None, axis...]
    ppermute x78, waiting for transfers between devices: 39.3 us -> 62.8 us  [extended(): lax.ppermute(lax.slice_in_dim(block, block.shape[dim] - width, None, axis...]
  transfers between devices with their start and end apart: 156 -> 156, of which waited for: 111 -> 94; matrix products, arithmetic and copies ran while one was open for 3% -> 3% of each run, Pallas kernels for 0% -> 0%
where the time goes in v1:
time: 1090 us; the launch traced here: 1080 us
  starting transfers between devices  369 us (34%)
  blocking collectives  303 us (28%)
  waiting for transfers between devices  198 us (18%)
  local copies, waits for them, and re-layouts  131 us (12%)
  other arithmetic  74.1 us (7%)
    ppermute x78, starting transfers between devices, extended(): lax.ppermute(lax.slice_in_dim(block, block.shape[dim] - width, None, axis...  268 us
    ppermute x78, waiting for transfers between devices, extended(): lax.ppermute(lax.slice_in_dim(block, 0, width, axis=dim), axis, backward)  135 us
    ppermute x78, starting transfers between devices, extended(): lax.ppermute(lax.slice_in_dim(block, 0, width, axis=dim), axis, backward)  101 us
    unnamed x2, blocking collectives  91.2 us
    all_gather x2, blocking collectives, coarsest(): lax.all_gather(rhs_field[None], ('gx', 'gy', 'gz'), axis=0, tiled=True)  85 us
    ppermute x78, waiting for transfers between devices, extended(): lax.ppermute(lax.slice_in_dim(block, block.shape[dim] - width, None, axis...  62.8 us
    all_gather x1, blocking collectives, per_device(): lax.all_gather(diagonals[LEVELS][None], ('gx', 'gy', 'gz'), axis=0, tiled...  44.6 us
    psum x1, blocking collectives, per_device(): lax.psum(local_dot(search, operated), ('gx', 'gy', 'gz'))  43.2 us
  transfers between devices with their start and end apart: 156, of which 94 were waited for; matrix products, arithmetic and copies ran while one was open for 3% of the time, Pallas kernels for 0%

profile of v1, /device:TPU:0, one launch (start us, length us, event | category | flops | bytes accessed | tf_op | source)
XLA Modules:
  0.0 1079.8 jit_solution(1633845646444769847)
XLA Ops:
  4.0 4.9 collective-permute-start.1
  11.3 4.6 collective-permute-start.2
  30.8 4.5 collective-permute-start.7
  43.0 9.7 reshape.128
  64.5 8.8 copy.1882
  73.3 11.7 %reduce_sum.144 = f32[4,8,8,64]{0,3,2,1:T(8,128)S(1)} reduce(f32[4,8,2,8,2,64,2]{0,6,5,4,3,2,1:T(2,128)} %bitcast.21, f32[]{:T(128)} %constant.28.clone.1), dimensions={2,4,6}, to_apply=%region_0.0 | reduce | flops 114688 | bytes 589828 | tf_op jit(solution)/shard_map/reduce_sum | solution.py:38
  87.1 4.5 collective-permute-start.13
  93.2 4.6 collective-permute-start.14
  100.6 4.6 collective-permute-done.15
  113.6 4.5 collective-permute-start.19
  126.0 4.4 collective-permute-done.21
  132.0 4.8 collective-permute-start.23
  146.1 4.2 collective-permute-done.24
  154.4 4.3 collective-permute-done.27
  161.0 4.6 collective-permute-start.29
  170.1 44.6 %all-gather.1 = f32[64,2,16]{2,1,0:T(2,128)S(1)} all-gather(f32[2,2,16]{2,1,0:T(2,128)S(1)} %multiply_add_fusion.3), channel_id=3, replica_groups=mesh['gx'=2,'gy'=4,'gz'=4] {'gx','gy','gz'}, dimensions={0}, use_global_device_ids=true | all-gather | bytes 8448 | tf_op jit(solution)/shard_map/all_gather | solution.py:106
  218.4 4.2 collective-permute-done.33
  229.9 40.5 %all-gather = f32[128,2,2,16]{3,2,1,0:T(2,128)S(1)} all-gather(f32[4,2,2,16]{3,2,1,0:T(2,128)S(1)} %copy.1905), channel_id=2, replica_groups=mesh['gx'=2,'gy'=4,'gz'=4] {'gx','gy','gz'}, dimensions={0}, use_global_device_ids=true | all-gather | bytes 33792 | tf_op jit(solution)/shard_map/all_gather | solution.py:113
  272.0 4.5 collective-permute-start.37
  278.4 4.2 collective-permute-done.36
  285.8 4.3 collective-permute-done.39
  308.7 4.3 collective-permute-done.45
  323.6 4.5 collective-permute-start.49
  335.0 4.7 collective-permute-done.51
  347.0 4.5 collective-permute-start.55
  357.9 4.4 collective-permute-done.57
  371.5 7.8 broadcast_in_dim.14
  379.3 10.0 copy.1931
  390.7 4.5 collective-permute-start.61
  408.5 4.6 collective-permute-start.65
  416.3 4.5 collective-permute-start.67
  434.0 5.1 collective-permute-start.71
  442.3 4.8 collective-permute-start.73
  460.0 5.1 collective-permute-start.77
  467.3 45.6 %all-reduce.16 = (f32[128]{0:T(128)S(1)}, f32[4]{0:T(128)S(1)}) all-reduce(f32[128]{0:T(128)S(1)} %dynamic-update-slice, f32[4]{0:T(128)S(1)} %get-tuple-element.12), channel_id=4, replica_groups=mesh['gx'=2,'gy'=4,'gz'=4] {'gx','gy','gz'}, use_global_device_ids=true, to_apply=%add.14 | all-reduce | flops 132 | bytes 1056
  514.9 4.5 collective-permute-start.79
  541.4 4.5 collective-permute-start.85
  553.1 4.3 collective-permute-done.87
  565.6 8.8 copy.1982
  574.3 13.1 %reduce_sum.153 = f32[4,8,8,64]{0,3,2,1:T(8,128)} reduce(f32[4,8,2,8,2,64,2]{0,6,5,4,3,2,1:T(2,128)} %bitcast.23, f32[]{:T(128)} %constant.28.clone.1), dimensions={2,4,6}, to_apply=%region_10.11 | reduce | flops 114688 | bytes 589828 | tf_op jit(solution)/shard_map/reduce_sum | solution.py:38
  591.1 4.5 collective-permute-start.91
  601.6 4.4 collective-permute-done.93
  607.6 4.7 collective-permute-start.95
  614.8 4.5 collective-permute-start.97
  625.9 4.4 collective-permute-done.99
  631.8 4.7 collective-permute-start.101
  657.8 4.3 collective-permute-done.105
  664.5 5.3 collective-permute-start.107
  686.5 4.3 collective-permute-done.111
  693.2 4.3 collective-permute-start.113
  701.9 44.5 %all-gather.3 = f32[128,2,2,16]{3,2,1,0:T(2,128)S(1)} all-gather(f32[4,2,2,16]{3,2,1,0:T(2,128)S(1)} %copy.2005), channel_id=5, replica_groups=mesh['gx'=2,'gy'=4,'gz'=4] {'gx','gy','gz'}, dimensions={0}, use_global_device_ids=true | all-gather | bytes 33792 | tf_op jit(solution)/shard_map/all_gather | solution.py:113
  759.5 4.3 collective-permute-done.117
  785.9 4.3 collective-permute-done.123
  806.3 4.5 collective-permute-start.127
  830.6 4.5 collective-permute-start.133
  855.3 8.9 broadcast_in_dim.17
  864.2 10.0 copy.2029
  875.6 4.5 collective-permute-start.139
  899.8 4.5 collective-permute-start.145
  917.3 4.2 collective-permute-start.149
  923.7 45.6 %all-reduce.15 = f32[128]{0:T(128)S(1)} all-reduce(f32[128]{0:T(128)S(1)} %dynamic-update-slice.1), channel_id=6, replica_groups=mesh['gx'=2,'gy'=4,'gz'=4] {'gx','gy','gz'}, use_global_device_ids=true, to_apply=%add.15 | all-reduce | flops 128 | bytes 1024
  970.9 4.5 collective-permute-start.151
  995.4 43.2 %psum.22 = f32[4]{0:T(128)S(1)} all-reduce(f32[4]{0:T(128)S(1)} %get-tuple-element.16), channel_id=1, replica_groups=mesh['gx'=2,'gy'=4,'gz'=4] {'gx','gy','gz'}, use_global_device_ids=true, to_apply=%region_16.17 | all-reduce | flops 4 | bytes 32 | tf_op jit(solution)/shard_map/psum | solution.py:161
  1039.7 39.3 %psum.23 = f32[4]{0:T(128)S(1)} all-reduce(f32[4]{0:T(128)S(1)} %get-tuple-element.199), channel_id=1, replica_groups=mesh['gx'=2,'gy'=4,'gz'=4] {'gx','gy','gz'}, use_global_device_ids=true, to_apply=%region_18.19 | all-reduce | flops 4 | bytes 32 | tf_op jit(solution)/shard_map/psum | solution.py:169
  (663 shorter events, 466.5 us)
Async XLA Ops:
  2.7 6.2 collective-permute-start
  4.0 6.5 collective-permute-start.1
  11.3 6.4 collective-permute-start.2
  30.8 6.1 collective-permute-start.7
  37.7 19.0 %collective-permute-start.8 = (f32[4,18,16,1]{1,2,3,0:T(8,128)S(1)}, f32[4,18,16,1]{1,2,3,0:T(8,128)S(1)}, u32[]{:S(2)}, u32[]{:S(2)}) collective-permute-start(f32[4,18,16,1]{1,2,3,0:T(8,128)S(1)} %copy.1872), channel_id=1, source_target_pairs={{0,4},{4,8},{8,12},{1,5},{5,9},{9,13},{2,6},{6,10},{10,14},{3,7},{... | collective-permute-start | bytes 13832 | tf_op jit(solution)/shard_map/ppermute | solution.py:17
  41.7 15.6 %collective-permute-start.9 = (f32[4,18,16,1]{1,2,3,0:T(8,128)S(1)}, f32[4,18,16,1]{1,2,3,0:T(8,128)S(1)}, u32[]{:S(2)}, u32[]{:S(2)}) collective-permute-start(f32[4,18,16,1]{1,2,3,0:T(8,128)S(1)} %copy.1873), channel_id=1, source_target_pairs={{4,0},{8,4},{12,8},{5,1},{9,5},{13,9},{6,2},{10,6},{14,10},{7,3},{... | collective-permute-start | bytes 13832 | tf_op jit(solution)/shard_map/ppermute | solution.py:20
  87.1 6.0 collective-permute-start.13
  93.2 7.4 collective-permute-start.14
  97.7 7.4 collective-permute-start.15
  111.9 6.3 collective-permute-start.18
  113.6 6.0 collective-permute-start.19
  119.7 6.3 collective-permute-start.20
  123.2 7.2 collective-permute-start.21
  130.7 6.1 collective-permute-start.22
  144.1 6.2 collective-permute-start.24
  152.7 6.0 collective-permute-start.27
  159.8 6.4 collective-permute-start.28
  166.9 48.1 %collective-permute-start.31 = (f32[4,1,4,32]{0,3,2,1:T(8,128)S(1)}, f32[4,1,4,32]{0,3,2,1:T(8,128)S(1)}, u32[]{:S(2)}, u32[]{:S(2)}) collective-permute-start(f32[4,1,4,32]{0,3,2,1:T(8,128)S(1)} %get-tuple-element.127), channel_id=1, source_target_pairs={{0,16},{1,17},{2,18},{3,19},{4,20},{5,21},{6,22},{7,23},{8,24},{9,... | collective-permute-start | bytes 6152 | tf_op jit(solution)/shard_map/ppermute | solution.py:17
  168.8 46.4 %collective-permute-start.30 = (f32[4,1,4,32]{0,3,2,1:T(8,128)S(1)}, f32[4,1,4,32]{0,3,2,1:T(8,128)S(1)}, u32[]{:S(2)}, u32[]{:S(2)}) collective-permute-start(f32[4,1,4,32]{0,3,2,1:T(8,128)S(1)} %get-tuple-element.128), channel_id=1, source_target_pairs={{16,0},{17,1},{18,2},{19,3},{20,4},{21,5},{22,6},{23,7},{24,8},{25... | collective-permute-start | bytes 6152 | tf_op jit(solution)/shard_map/ppermute | solution.py:20
  216.6 6.0 collective-permute-start.33
  272.0 6.3 collective-permute-start.37
  276.4 6.2 collective-permute-start.36
  284.1 6.0 collective-permute-start.39
  298.5 6.6 collective-permute-start.42
  306.9 6.0 collective-permute-start.45
  323.6 6.0 collective-permute-start.49
  331.6 8.1 collective-permute-start.51
  355.0 7.2 collective-permute-start.57
  390.7 6.1 collective-permute-start.61
  416.3 6.1 collective-permute-start.67
  432.7 6.4 collective-permute-start.70
  441.0 6.1 collective-permute-start.72
  442.3 6.1 collective-permute-start.73
  458.7 6.5 collective-permute-start.76
  460.0 6.0 collective-permute-start.77
  514.9 6.1 collective-permute-start.79
  541.4 6.1 collective-permute-start.85
  551.3 6.1 collective-permute-start.87
  598.8 7.2 collective-permute-start.93
  623.1 7.2 collective-permute-start.99
  630.5 6.0 collective-permute-start.100
  646.8 6.2 collective-permute-start.102
  656.0 6.0 collective-permute-start.105
  663.2 8.5 collective-permute-start.106
  664.5 7.8 collective-permute-start.107
  675.6 6.2 collective-permute-start.108
  684.8 6.0 collective-permute-start.111
  691.9 6.8 collective-permute-start.112
  749.4 6.2 collective-permute-start.114
  757.7 6.0 collective-permute-start.117
  764.9 7.1 collective-permute-start.118
  766.1 6.4 collective-permute-start.119
  775.6 6.2 collective-permute-start.120
  784.2 6.0 collective-permute-start.123
  791.3 6.9 collective-permute-start.124
  792.6 6.3 collective-permute-start.125
  812.4 7.0 collective-permute-start.128
  815.6 7.8 collective-permute-start.129
  836.7 6.6 collective-permute-start.134
  838.9 8.5 collective-permute-start.135
  875.6 6.1 collective-permute-start.139
  885.2 6.0 collective-permute-start.141
  899.8 6.1 collective-permute-start.145
  970.9 6.1 collective-permute-start.151
  (112 other events, 780.3 us)
